TPU v7x, 256 devices: a whole 4x4x8 slice. The times are simulated.
256 devices in a mesh: gx: 4 (over y), gy: 8 (over x, core), gz: 8 (over z).
Axes of the slice: x: 4, y: 4, z: 8, core: 2. Of those that a mesh axis runs over, the one named last changes fastest.
Arguments:
- positions: float32 [3, 32768, 128], P(None, ('gx', 'gy', 'gz')), may hold values from 0 to 1, as said below
- charges: float32 [32768, 128], P(('gx', 'gy', 'gz')), may hold values from -6 to 6
- velocities: float32 [3, 32768, 128], P(None, ('gx', 'gy', 'gz')), may hold values from -6 to 6
- leaf_ids: int32 [32768], P(('gx', 'gy', 'gz')), may hold values from 0 to 2097151, as said below
- live_counts: int32 [256], replicated, may hold values from 32 to 96
- send_counts: int32 [8, 256], replicated, may hold values from 0 to 32, as said below
Outputs:
- moved_positions: float32 [3, 32768, 128], P(None, ('gx', 'gy', 'gz'))
- moved_charges: float32 [32768, 128], P(('gx', 'gy', 'gz'))
- moved_velocities: float32 [3, 32768, 128], P(None, ('gx', 'gy', 'gz'))
- moved_leaves: int32 [32768], P(('gx', 'gy', 'gz'))
- leaf_moments: float32 [286, 32768], P(None, ('gx', 'gy', 'gz'))
- parent_moments: float32 [286, 32768], P(None, ('gx', 'gy', 'gz'))
Inputs may be any that keep to these rules, and one draw needn't show every extreme that they name: `positions`: every particle of a live slot lies inside the leaf cell of side 2^-7 named by the slot's leaf index. `leaf_ids`: morton indices of cells at depth 7; a leaf's parent cell is its index // 8. `send_counts`: no device sends more blocks than it holds live; after every section no device holds more than 128 live blocks; in every draw some device sends exactly 32 blocks in the first section and its partner then holds exactly 128.
All inputs are finite; a program needn't handle non-finite values.
Results may differ from a plain program's by a relative error of at most 0.0003.
Values sent between devices are 32-bit elements; how exact they have to be, the bound alone decides.
A program may use at most 128 MiB of HBM per device.

v0:
```python
import functools
import math

import jax
import jax.numpy as jnp
import numpy as np
from jax import lax
from jax.experimental import pallas as pl
from jax.experimental.pallas import tpu as pltpu
from jax.sharding import PartitionSpec as P

ORDER = 10
LEVEL = 7
CAP = 128
SLAB = 32
COMPS = 8
CHUNKS = 2
PER = COMPS // CHUNKS
MESH = pl.DeviceIdType.MESH

PHASES = (
    ("gx", (2, 1), 0),
    ("gy", (4, 2), 2),
    ("gy", (1,), 4),
    ("gz", (4, 2), 5),
    ("gz", (1,), 7),
)
SIZES = {"gx": 4, "gy": 8, "gz": 8}
STRIDES = {"gx": 64, "gy": 8, "gz": 1}
FRAMES = [(p, slot) for p, phase in enumerate(PHASES) for slot in range(2 ** len(phase[1]) - 1)]
LIST_BASE = 64
FP_BASE = 160
X_BASE = 128
FR_BASE = 32

TRIPLES = [
    (p, q, r)
    for p in range(ORDER + 1)
    for q in range(ORDER + 1 - p)
    for r in range(ORDER + 1 - p - q)
]
NCOEF = len(TRIPLES)
ROWS = 288


def bit_of(value, mask):
    return (value // mask) % 2


def flipped(value, mask):
    for one in (1, 2, 4):
        if mask & one:
            value = value + one - 2 * one * bit_of(value, one)
    return value


def pick(bit, one, zero):
    return bit * one + (1 - bit) * zero


def exchange(live, sends, leaves, positions, charges, velocities, final,
             list_a, list_b, frame_p, frame_r, frame_x, out, land,
             send_sem, recv_sem):
    where = {axis: lax.axis_index(axis) for axis in SIZES}

    def device(coords):
        return sum(coords[axis] * STRIDES[axis] for axis in SIZES)

    def moved(coords, axis, mask):
        return {**coords, axis: flipped(coords[axis], mask)}

    barrier = pltpu.get_barrier_semaphore()
    partners = 0
    for axis, masks, _ in PHASES:
        for mask in masks + ((sum(masks),) if len(masks) == 2 else ()):
            pl.semaphore_signal(
                barrier, inc=1, device_id={axis: flipped(where[axis], mask)}, device_id_type=MESH
            )
            partners += 1

    def section_step(coords, count, section, axis, mask):
        sent = sends[section, device(coords)]
        got = sends[section, device(moved(coords, axis, mask))]
        return sent, got, count - sent + got

    def start_count(coords, phase_now):
        count = live[device(coords)]
        for axis, masks, section in PHASES[:phase_now]:
            for step, mask in enumerate(masks):
                count = section_step(coords, count, section + step, axis, mask)[2]
        return count

    plans = []
    count = live[device(where)]
    for phase_now, (axis, masks, section) in enumerate(PHASES):
        plan = {}
        m1 = masks[0]
        a = bit_of(where[axis], m1)
        sent, got, count1 = section_step(where, count, section, axis, m1)
        kept = count - sent
        plan["start_a"] = pick(a, 0, kept)
        fs = pick(a, 0, kept)
        dl = pick(a, sent - got, 0)
        plan["got"] = got
        if len(masks) == 2:
            m2 = masks[1]
            b = bit_of(where[axis], m2)
            sent1, got1, count2 = section_step(where, count1, section + 1, axis, m2)
            kept1 = count1 - sent1
            start_b = pick(b, 0, kept1)
            plan["start_q"] = start_b + dl
            d1 = pick(b, sent1 - got1, 0)
            xs = pick(b, 0, kept1)
            plan["fs"] = fs - d1
            plan["list_off"] = dl + d1
            plan["xs"] = xs
            plan["xe"] = xs + got1
            other = moved(where, axis, m2)
            count_q = start_count(other, phase_now)
            sent_q, got_q, count1_q = section_step(other, count_q, section, axis, m1)
            fs_q = pick(a, 0, count_q - sent_q)
            start_bq = pick(b, count1_q - got1, 0)
            off_r = start_bq - fs_q
            plan["off_r"] = jnp.maximum(jnp.minimum(off_r, SLAB), -SLAB)
            plan["got_q"] = got_q
            count = count2
        else:
            plan["fs"] = fs
            plan["list_off"] = dl
            count = count1
        plan["fe"] = plan["fs"] + got
        plan["count"] = count
        plans.append(plan)

    for axis in range(3):
        list_a[axis, LIST_BASE : LIST_BASE + CAP] = positions[axis]
        list_a[4 + axis, LIST_BASE : LIST_BASE + CAP] = velocities[axis]
    list_a[3, LIST_BASE : LIST_BASE + CAP] = charges[...]
    list_a[7, LIST_BASE : LIST_BASE + CAP] = jnp.broadcast_to(
        leaves[...].astype(jnp.float32), (CAP, 128)
    ).T
    lists = (list_a, list_b)

    def transfers(p, j):
        axis, masks, _ = PHASES[p]
        rows = slice(PER * j, PER * (j + 1))
        todo = [(0, 0, masks[0])]
        if len(masks) == 2:
            todo += [(1, 1, masks[1]), (2, 0, masks[0] + masks[1])]
        copies = []
        for slot, source, mask in todo:
            at = FRAMES.index((p, slot)) * CHUNKS + j
            copies.append(
                pltpu.make_async_remote_copy(
                    src_ref=out.at[2 * p + source, rows],
                    dst_ref=land.at[3 * p + slot, rows],
                    send_sem=send_sem.at[at],
                    recv_sem=recv_sem.at[at],
                    device_id={axis: flipped(where[axis], mask)},
                    device_id_type=MESH,
                )
            )
        return copies

    started = {}

    def send(p, j):
        now, plan = lists[p % 2], plans[p]
        for k in range(PER * j, PER * (j + 1)):
            out[2 * p, k] = now[k, pl.ds(LIST_BASE + plan["start_a"], SLAB), :]
            if "start_q" in plan:
                out[2 * p + 1, k] = now[k, pl.ds(LIST_BASE + plan["start_q"], SLAB), :]
        started[p, j] = transfers(p, j)
        for copy in started[p, j]:
            copy.start()

    def receive(p, j):
        now, plan = lists[p % 2], plans[p]
        last = p == len(PHASES) - 1
        for copy in started[p, j]:
            copy.wait_recv()
        two = "start_q" in plan
        for k in range(PER * j, PER * (j + 1)):
            frame_p[k, FP_BASE : FP_BASE + SLAB] = land[3 * p, k]
            if two:
                frame_r[k, FR_BASE : FR_BASE + SLAB] = land[3 * p + 2, k]
        if two:
            row = lax.broadcasted_iota(jnp.int32, (SLAB, 128), 0) + plan["off_r"]
            from_r = (row >= 0) & (row < plan["got_q"])
            for k in range(PER * j, PER * (j + 1)):
                frame_x[k, X_BASE : X_BASE + SLAB] = jnp.where(
                    from_r,
                    frame_r[k, pl.ds(FR_BASE + plan["off_r"], SLAB), :],
                    land[3 * p + 1, k],
                )

        def tile(t, carry):
            base = t * 8
            row = lax.broadcasted_iota(jnp.int32, (8, 128), 0) + base
            from_p = (row >= plan["fs"]) & (row < plan["fe"])
            if two:
                from_x = (row >= plan["xs"]) & (row < plan["xe"])
            if last:
                full = row < plan["count"]
            for k in range(PER * j, PER * (j + 1)):
                value = jnp.where(
                    from_p,
                    frame_p[k, pl.ds(FP_BASE - plan["fs"] + base, 8), :],
                    now[k, pl.ds(LIST_BASE + plan["list_off"] + base, 8), :],
                )
                if two:
                    value = jnp.where(
                        from_x, frame_x[k, pl.ds(X_BASE - plan["xs"] + base, 8), :], value
                    )
                if last:
                    final[k, pl.ds(base, 8), :] = jnp.where(full, value, -1.0 if k == 7 else 0.0)
                else:
                    lists[(p + 1) % 2][k, pl.ds(LIST_BASE + base, 8), :] = value
            return carry

        lax.fori_loop(0, CAP // 8, tile, 0, unroll=True)

    pl.semaphore_wait(barrier, partners)
    for j in range(CHUNKS):
        send(0, j)
    for t in range(len(PHASES) + CHUNKS - 1):
        for j in reversed(range(CHUNKS)):
            p = t - j
            if 0 <= p < len(PHASES):
                receive(p, j)
                if p + 1 < len(PHASES):
                    send(p + 1, j)
    for copies in started.values():
        for copy in copies:
            copy.wait_send()


def shift_table():
    table = np.zeros((ROWS, ROWS), np.float32)
    for k, (p, q, r) in enumerate(TRIPLES):
        for j, (e, f, g) in enumerate(TRIPLES):
            if e <= p and f <= q and g <= r:
                table[k, j] = (
                    math.comb(p, e) * math.comb(q, f) * math.comb(r, g) * 0.5 ** (p + q + r)
                )
    return jnp.asarray(table, jnp.bfloat16)


def split3(value):
    high = value.astype(jnp.bfloat16)
    rest = value - high.astype(jnp.float32)
    middle = rest.astype(jnp.bfloat16)
    low = (rest - middle.astype(jnp.float32)).astype(jnp.bfloat16)
    return high, middle, low


def dot32(left, right):
    return jnp.dot(left, right, preferred_element_type=jnp.float32)


def moments(final, table, positions, charges, velocities, leaves, leaf_out, parent_out,
            u_ref, v_ref, w_ref, a_ref, b_ref, flip_ref, sign_ref, copy_sem):
    copies = [
        pltpu.make_async_copy(final.at[0:3], positions, copy_sem.at[0]),
        pltpu.make_async_copy(final.at[3], charges, copy_sem.at[1]),
        pltpu.make_async_copy(final.at[4:7], velocities, copy_sem.at[2]),
    ]
    for copy in copies:
        copy.start()
    leaf_rows = final[7]
    leaf_row = leaf_rows.T[0:8].astype(jnp.int32)
    leaves[...] = leaf_row[0:1]
    live_row = leaf_row >= 0
    leaf = jnp.where(live_row, leaf_row, 0)
    cells = []
    for axis_bit in (2, 1, 0):
        cell = jnp.zeros_like(leaf)
        for level in range(LEVEL):
            cell = cell + ((leaf >> (3 * level + axis_bit)) & 1) * 2**level
        cells.append(cell[0:1].astype(jnp.float32))
    for axis, ref in enumerate((u_ref, v_ref, w_ref)):
        ref[...] = 2.0 * (final[axis].T * float(2**LEVEL) - cells[axis]) - 1.0
    a_ref[...] = final[3].T * (1.0 / 16.0)
    flips = [
        jnp.where(((leaf >> bit) & 1)[0:1] == 1, 1.0, -1.0).astype(jnp.float32) for bit in (2, 1, 0)
    ]
    signs = {}
    for code in range(8):
        sign = jnp.ones((1, 128), jnp.float32)
        for axis in range(3):
            if code >> (2 - axis) & 1:
                sign = sign * flips[axis]
        signs[code] = sign
    flip_ref[280:288] = jnp.zeros((8, 128), jnp.float32)
    sign_ref[280:288] = jnp.zeros((8, 128), jnp.float32)
    step = 8
    k = 0
    for p in range(ORDER + 1):
        for q in range(ORDER + 1 - p):
            count = ORDER + 1 - p - q

            def body(g, sums, first=q == 0, more_q=q < ORDER - p, more_p=p < ORDER, count=count):
                sums = list(sums)
                for i in range(step):
                    rows = pl.ds((g * step + i) * 8, 8)
                    term = (a_ref if first else b_ref)[rows, :]
                    if more_q:
                        b_ref[rows, :] = term * v_ref[rows, :]
                    if first and more_p:
                        a_ref[rows, :] = term * u_ref[rows, :]
                    w = w_ref[rows, :]
                    for r in range(count):
                        sums[r] = sums[r] + term
                        if r + 1 < count:
                            term = term * w
                return tuple(sums)

            zero = jnp.zeros((8, 128), jnp.float32)
            sums = lax.fori_loop(0, 16 // step, body, (zero,) * count)
            for r in range(count):
                row = jnp.sum(sums[r], axis=0, keepdims=True)
                leaf_out[k : k + 1] = row
                sign = signs[(p & 1) << 2 | (q & 1) << 1 | (r & 1)]
                flip_ref[k : k + 1] = row * sign
                sign_ref[k : k + 1] = sign
                k += 1
    high, middle, low = split3(flip_ref[...])
    matrix = table[...]
    shifted = (dot32(matrix, low) + dot32(matrix, middle)) + dot32(matrix, high)
    shifted = shifted * sign_ref[...]
    leaf_col = leaf_rows.astype(jnp.int32)
    sibling = (
        ((leaf_col >> 3) == (leaf_row >> 3)[0:1]) & (leaf_col >= 0) & live_row[0:1]
    ).astype(jnp.float32).astype(jnp.bfloat16)
    high, middle, low = split3(shifted)
    total = (dot32(low, sibling) + dot32(middle, sibling)) + dot32(high, sibling)
    parent_out[...] = total[:NCOEF]
    for copy in copies:
        copy.wait()


def per_device(positions, charges, velocities, leaf_ids, live_counts, send_counts):
    vmem = pl.BlockSpec(memory_space=pltpu.VMEM)
    smem = pl.BlockSpec(memory_space=pltpu.SMEM)
    anywhere = pl.BlockSpec(memory_space=pl.ANY)
    f32 = jnp.float32
    copies = len(FRAMES) * CHUNKS
    final = pl.pallas_call(
        exchange,
        name="exchange",
        out_shape=jax.ShapeDtypeStruct((COMPS, CAP, 128), f32),
        in_specs=[smem, smem, vmem, vmem, vmem, vmem],
        out_specs=vmem,
        scratch_shapes=[
            pltpu.VMEM((COMPS, LIST_BASE + CAP + 64, 128), f32),
            pltpu.VMEM((COMPS, LIST_BASE + CAP + 64, 128), f32),
            pltpu.VMEM((COMPS, FP_BASE + CAP + 64, 128), f32),
            pltpu.VMEM((COMPS, FR_BASE + 2 * SLAB, 128), f32),
            pltpu.VMEM((COMPS, X_BASE + CAP, 128), f32),
            pltpu.VMEM((2 * len(PHASES), COMPS, SLAB, 128), f32),
            pltpu.VMEM((3 * len(PHASES), COMPS, SLAB, 128), f32),
            pltpu.SemaphoreType.DMA((copies,)),
            pltpu.SemaphoreType.DMA((copies,)),
        ],
        compiler_params=pltpu.CompilerParams(
            collective_id=0, has_side_effects=True, vmem_limit_bytes=24 * 2**20
        ),
    )(live_counts, send_counts, leaf_ids.reshape(1, CAP), positions, charges, velocities)

    square = pltpu.VMEM((CAP, 128), f32)
    outs = pl.pallas_call(
        moments,
        name="moments",
        out_shape=(
            jax.ShapeDtypeStruct((3, CAP, 128), f32),
            jax.ShapeDtypeStruct((CAP, 128), f32),
            jax.ShapeDtypeStruct((3, CAP, 128), f32),
            jax.ShapeDtypeStruct((1, CAP), jnp.int32),
            jax.ShapeDtypeStruct((NCOEF, CAP), f32),
            jax.ShapeDtypeStruct((NCOEF, CAP), f32),
        ),
        in_specs=[vmem, vmem],
        out_specs=(anywhere, anywhere, anywhere, vmem, vmem, vmem),
        scratch_shapes=[square] * 5
        + [
            pltpu.VMEM((ROWS, 128), f32),
            pltpu.VMEM((ROWS, 128), f32),
            pltpu.SemaphoreType.DMA((3,)),
        ],
        compiler_params=pltpu.CompilerParams(vmem_limit_bytes=16 * 2**20),
    )(final, shift_table())
    moved_positions, moved_charges, moved_velocities, moved_leaves, leaf_part, parent_part = outs
    return (
        moved_positions,
        moved_charges,
        moved_velocities,
        moved_leaves.reshape(CAP),
        leaf_part,
        parent_part,
    )


def solution(mesh):
    names = ("gx", "gy", "gz")
    in_specs = (P(None, names, None), P(names, None), P(None, names, None), P(names), P(), P())
    out_specs = (
        P(None, names, None),
        P(names, None),
        P(None, names, None),
        P(names),
        P(None, names),
        P(None, names),
    )
    return jax.shard_map(
        per_device, mesh=mesh, in_specs=in_specs, out_specs=out_specs, check_vma=False
    )
```

profile of v0, /device:TPU:1, one launch (start us, length us, event | category | flops | bytes accessed | tf_op | source)
XLA Modules:
  0.0 49.9 jit_solution(14288652100285647195)
XLA Ops:
  0.6 0.0 copy-start.5
  0.6 0.0 copy-start.6
  0.7 0.7 %copy-done.5 = s32[256]{0:T(256)S(1)} copy-done((s32[256]{0:T(256)S(1)}, s32[256]{0:T(256)}, u32[]{:S(2)}) %copy-start.5) | copy-done | bytes 1048
  1.3 0.0 copy-done.6
  1.3 0.0 copy-start.1
  1.3 0.9 %copy-done.1 = f32[3,128,128]{2,1,0:T(8,128)S(1)} copy-done((f32[3,128,128]{2,1,0:T(8,128)S(1)}, f32[3,128,128]{2,1,0:T(8,128)}, u32[]{:S(2)}) %copy-start.1) | copy-done | bytes 196632
  2.2 0.0 copy-start.2
  2.2 0.9 %copy-done.2 = f32[3,128,128]{2,1,0:T(8,128)S(1)} copy-done((f32[3,128,128]{2,1,0:T(8,128)S(1)}, f32[3,128,128]{2,1,0:T(8,128)}, u32[]{:S(2)}) %copy-start.2) | copy-done | bytes 196632
  3.2 0.0 copy-start.3
  3.2 0.8 %copy-done.3 = f32[128,128]{1,0:T(8,128)S(1)} copy-done((f32[128,128]{1,0:T(8,128)S(1)}, f32[128,128]{1,0:T(8,128)}, u32[]{:S(2)}) %copy-start.3) | copy-done | bytes 65560
  4.0 0.0 copy-start.4
  4.0 0.7 %copy-done.4 = s32[8,256]{1,0:T(8,128)S(1)} copy-done((s32[8,256]{1,0:T(8,128)S(1)}, s32[8,256]{1,0:T(8,128)}, u32[]{:S(2)}) %copy-start.4) | copy-done | bytes 8216
  4.7 0.0 copy-start
  4.7 41.0 %exchange.1.final = f32[8,128,128]{2,1,0:T(8,128)S(1)} custom-call(s32[256]{0:T(256)S(1)} %copy-done.5, s32[8,256]{1,0:T(8,128)S(1)} %copy-done.4, s32[1,128]{1,0:T(1,128)S(1)} %bitcast.2, f32[3,128,128]{2,1,0:T(8,128)S(1)} %copy-done.1, f32[128,128]{1,0:T(8,128)S(1)} %copy-done.3, f32[3,128,128]{2,1,0:T(8,128)S(1)} %copy-done.2), custom_call_target="tpu_custom_call" | custom-call | tf_op jit(solution)/shard_map/exchange/pallas_call | solution.py:348
  45.8 0.0 copy-done
  45.8 4.1 %moments.1 = (f32[3,128,128]{2,1,0:T(8,128)}, f32[128,128]{1,0:T(8,128)}, f32[3,128,128]{2,1,0:T(8,128)}, s32[1,128]{1,0:T(1,128)}, f32[286,128]{1,0:T(8,128)}, /*index=5*/f32[286,128]{1,0:T(8,128)}) custom-call(f32[8,128,128]{2,1,0:T(8,128)S(1)} %exchange.1.final, bf16[288,288]{1,0:T(8,128)(2,1)S(1)} %copy-done), custom_call_target="tpu_custom_call" | custom-call | tf_op jit(solution)/shard_map/moments/pallas_call | solution.py:371
Async XLA Ops:
  0.6 0.7 %copy-start.5 = (s32[256]{0:T(256)S(1)}, s32[256]{0:T(256)}, u32[]{:S(2)}) copy-start(s32[256]{0:T(256)} %live.1) | copy-start | bytes 3076
  0.6 0.7 %copy-start.6 = (s32[128]{0:T(128)S(1)}, s32[128]{0:T(128)}, u32[]{:S(2)}) copy-start(s32[128]{0:T(128)} %param.10) | copy-start | bytes 1540
  1.3 0.9 %copy-start.1 = (f32[3,128,128]{2,1,0:T(8,128)S(1)}, f32[3,128,128]{2,1,0:T(8,128)}, u32[]{:S(2)}) copy-start(f32[3,128,128]{2,1,0:T(8,128)} %positions.1) | copy-start | bytes 589828
  2.2 0.9 %copy-start.2 = (f32[3,128,128]{2,1,0:T(8,128)S(1)}, f32[3,128,128]{2,1,0:T(8,128)}, u32[]{:S(2)}) copy-start(f32[3,128,128]{2,1,0:T(8,128)} %velocities.1) | copy-start | bytes 589828
  3.2 0.8 %copy-start.3 = (f32[128,128]{1,0:T(8,128)S(1)}, f32[128,128]{1,0:T(8,128)}, u32[]{:S(2)}) copy-start(f32[128,128]{1,0:T(8,128)} %charges.1) | copy-start | bytes 196612
  4.0 0.7 %copy-start.4 = (s32[8,256]{1,0:T(8,128)S(1)}, s32[8,256]{1,0:T(8,128)}, u32[]{:S(2)}) copy-start(s32[8,256]{1,0:T(8,128)} %sends.1) | copy-start | bytes 24580
  4.7 41.1 %copy-start = (bf16[288,288]{1,0:T(8,128)(2,1)S(1)}, bf16[288,288]{1,0:T(8,128)(2,1)}, u32[]{:S(2)}) copy-start(bf16[288,288]{1,0:T(8,128)(2,1)} %constant.2.clone.table) | copy-start | bytes 497668
where the time goes:
time: 50.1 us; the launch traced here: 49.9 us
  Pallas kernels  45.2 us (90%)
  local copies, waits for them, and re-layouts  4.06 us (8%)
  between operations  0.67 us (1%)
    pallas_call x1, Pallas kernels, per_device(): pl.pallas_call(exchange, name='exchange', out_shape=jax.ShapeDtypeStruct(...  41 us
    pallas_call x1, Pallas kernels, per_device(): pl.pallas_call(moments, name='moments', out_shape=(jax.ShapeDtypeStruct((...  4.12 us
    unnamed x14, local copies, waits for them, and re-layouts  4.06 us

commit v1 on v0

--- a/solution.py
+++ b/solution.py
@@ -13,9 +13,10 @@
 LEVEL = 7
 CAP = 128
 SLAB = 32
-COMPS = 8
-CHUNKS = 2
-PER = COMPS // CHUNKS
+COMPS = 7
+FRAME = SLAB * COMPS + 8
+LEAF_ROWS = slice(SLAB * COMPS, FRAME)
+CHUNKS = ((0, 2), (2, 5), (5, 7))
 MESH = pl.DeviceIdType.MESH
 
 PHASES = (
@@ -28,6 +29,13 @@
 SIZES = {"gx": 4, "gy": 8, "gz": 8}
 STRIDES = {"gx": 64, "gy": 8, "gz": 1}
 FRAMES = [(p, slot) for p, phase in enumerate(PHASES) for slot in range(2 ** len(phase[1]) - 1)]
+VMEM_LIMIT = 24 * 2**20
+ORDER_OF_WORK = [
+    (t - j, j)
+    for t in range(len(PHASES) + len(CHUNKS) - 1)
+    for j in reversed(range(len(CHUNKS)))
+    if 0 <= t - j < len(PHASES)
+]
 LIST_BASE = 64
 FP_BASE = 160
 X_BASE = 128
@@ -43,40 +51,58 @@
 ROWS = 288
 
 
-def bit_of(value, mask):
-    return (value // mask) % 2
-
-
-def flipped(value, mask):
-    for one in (1, 2, 4):
-        if mask & one:
-            value = value + one - 2 * one * bit_of(value, one)
-    return value
+def bits_of(value):
+    high = jnp.where(value >= 4, 1, 0)
+    rest = value - 4 * high
+    middle = jnp.where(rest >= 2, 1, 0)
+    return {4: high, 2: middle, 1: rest - 2 * middle}
 
 
 def pick(bit, one, zero):
     return bit * one + (1 - bit) * zero
 
 
-def exchange(live, sends, leaves, positions, charges, velocities, final,
-             list_a, list_b, frame_p, frame_r, frame_x, out, land,
-             send_sem, recv_sem):
+def exchange(live_hbm, sends_hbm, leaves_hbm, positions, charges, velocities, final, leaf_final,
+             live, sends, leaves, list_a, list_b, frame_p, frame_r, frame_x, out, land,
+             load_sem, send_sem, recv_sem):
     where = {axis: lax.axis_index(axis) for axis in SIZES}
-
-    def device(coords):
-        return sum(coords[axis] * STRIDES[axis] for axis in SIZES)
-
-    def moved(coords, axis, mask):
-        return {**coords, axis: flipped(coords[axis], mask)}
+    bits = {axis: bits_of(where[axis]) for axis in SIZES}
+    me = sum(where[axis] * STRIDES[axis] for axis in SIZES)
+
+    def step_of(axis, mask):
+        return sum(m - 2 * m * bits[axis][m] for m in (4, 2, 1) if mask & m)
+
+    def peer(axis, mask):
+        return {axis: where[axis] + step_of(axis, mask)}
+
+    def device(flips):
+        return me + sum(step_of(axis, mask) * STRIDES[axis] for axis, mask in flips)
+
+    def moved(flips, axis, mask):
+        return flips ^ {(axis, mask)}
 
     barrier = pltpu.get_barrier_semaphore()
     partners = 0
     for axis, masks, _ in PHASES:
         for mask in masks + ((sum(masks),) if len(masks) == 2 else ()):
             pl.semaphore_signal(
-                barrier, inc=1, device_id={axis: flipped(where[axis], mask)}, device_id_type=MESH
+                barrier, inc=1, device_id=peer(axis, mask), device_id_type=MESH
             )
             partners += 1
+    lists = (list_a, list_b)
+    body = slice(LIST_BASE, LIST_BASE + CAP)
+    pairs = [(live_hbm, live), (sends_hbm, sends), (leaves_hbm, leaves)]
+    pairs += [(positions.at[k], list_a.at[k, body]) for k in range(3)]
+    pairs += [(charges, list_a.at[3, body])]
+    pairs += [(velocities.at[k], list_a.at[4 + k, body]) for k in range(3)]
+    loads = [
+        pltpu.make_async_copy(source, target, load_sem.at[k])
+        for k, (source, target) in enumerate(pairs)
+    ]
+    for load in loads:
+        load.start()
+    for load in loads[:2]:
+        load.wait()
 
     def section_step(coords, count, section, axis, mask):
         sent = sends[section, device(coords)]
@@ -91,21 +117,21 @@
         return count
 
     plans = []
-    count = live[device(where)]
+    here = frozenset()
+    count = live[device(here)]
     for phase_now, (axis, masks, section) in enumerate(PHASES):
         plan = {}
         m1 = masks[0]
-        a = bit_of(where[axis], m1)
-        sent, got, count1 = section_step(where, count, section, axis, m1)
+        a = bits[axis][m1]
+        sent, got, count1 = section_step(here, count, section, axis, m1)
         kept = count - sent
         plan["start_a"] = pick(a, 0, kept)
         fs = pick(a, 0, kept)
         dl = pick(a, sent - got, 0)
-        plan["got"] = got
         if len(masks) == 2:
             m2 = masks[1]
-            b = bit_of(where[axis], m2)
-            sent1, got1, count2 = section_step(where, count1, section + 1, axis, m2)
+            b = bits[axis][m2]
+            sent1, got1, count2 = section_step(here, count1, section + 1, axis, m2)
             kept1 = count1 - sent1
             start_b = pick(b, 0, kept1)
             plan["start_q"] = start_b + dl
@@ -115,7 +141,7 @@
             plan["list_off"] = dl + d1
             plan["xs"] = xs
             plan["xe"] = xs + got1
-            other = moved(where, axis, m2)
+            other = moved(here, axis, m2)
             count_q = start_count(other, phase_now)
             sent_q, got_q, count1_q = section_step(other, count_q, section, axis, m1)
             fs_q = pick(a, 0, count_q - sent_q)
@@ -132,44 +158,47 @@
         plan["count"] = count
         plans.append(plan)
 
-    for axis in range(3):
-        list_a[axis, LIST_BASE : LIST_BASE + CAP] = positions[axis]
-        list_a[4 + axis, LIST_BASE : LIST_BASE + CAP] = velocities[axis]
-    list_a[3, LIST_BASE : LIST_BASE + CAP] = charges[...]
-    list_a[7, LIST_BASE : LIST_BASE + CAP] = jnp.broadcast_to(
-        leaves[...].astype(jnp.float32), (CAP, 128)
-    ).T
-    lists = (list_a, list_b)
-
     def transfers(p, j):
         axis, masks, _ = PHASES[p]
-        rows = slice(PER * j, PER * (j + 1))
+        first, end = CHUNKS[j]
+        rows = slice(SLAB * first, SLAB * end + (8 if end == COMPS else 0))
         todo = [(0, 0, masks[0])]
         if len(masks) == 2:
             todo += [(1, 1, masks[1]), (2, 0, masks[0] + masks[1])]
         copies = []
         for slot, source, mask in todo:
-            at = FRAMES.index((p, slot)) * CHUNKS + j
+            at = FRAMES.index((p, slot)) * len(CHUNKS) + j
             copies.append(
                 pltpu.make_async_remote_copy(
                     src_ref=out.at[2 * p + source, rows],
                     dst_ref=land.at[3 * p + slot, rows],
                     send_sem=send_sem.at[at],
                     recv_sem=recv_sem.at[at],
-                    device_id={axis: flipped(where[axis], mask)},
+                    device_id=peer(axis, mask),
                     device_id_type=MESH,
                 )
             )
         return copies
 
     started = {}
+    leaf_list = {}
+
+    def to_left(row, amount):
+        return pltpu.roll(row, (4 * 128 - amount) % 128, 1)
 
     def send(p, j):
         now, plan = lists[p % 2], plans[p]
-        for k in range(PER * j, PER * (j + 1)):
-            out[2 * p, k] = now[k, pl.ds(LIST_BASE + plan["start_a"], SLAB), :]
-            if "start_q" in plan:
-                out[2 * p + 1, k] = now[k, pl.ds(LIST_BASE + plan["start_q"], SLAB), :]
+        first, end = CHUNKS[j]
+        two = "start_q" in plan
+        for k in range(first, end):
+            rows = slice(SLAB * k, SLAB * (k + 1))
+            out[2 * p, rows] = now[k, pl.ds(LIST_BASE + plan["start_a"], SLAB), :]
+            if two:
+                out[2 * p + 1, rows] = now[k, pl.ds(LIST_BASE + plan["start_q"], SLAB), :]
+        if end == COMPS:
+            out[2 * p, LEAF_ROWS] = to_left(leaf_list[p], plan["start_a"])
+            if two:
+                out[2 * p + 1, LEAF_ROWS] = to_left(leaf_list[p], plan["start_q"])
         started[p, j] = transfers(p, j)
         for copy in started[p, j]:
             copy.start()
@@ -177,21 +206,23 @@
     def receive(p, j):
         now, plan = lists[p % 2], plans[p]
         last = p == len(PHASES) - 1
+        first, end = CHUNKS[j]
         for copy in started[p, j]:
             copy.wait_recv()
         two = "start_q" in plan
-        for k in range(PER * j, PER * (j + 1)):
-            frame_p[k, FP_BASE : FP_BASE + SLAB] = land[3 * p, k]
+        for k in range(first, end):
+            rows = slice(SLAB * k, SLAB * (k + 1))
+            frame_p[k, FP_BASE : FP_BASE + SLAB] = land[3 * p, rows]
             if two:
-                frame_r[k, FR_BASE : FR_BASE + SLAB] = land[3 * p + 2, k]
+                frame_r[k, FR_BASE : FR_BASE + SLAB] = land[3 * p + 2, rows]
         if two:
             row = lax.broadcasted_iota(jnp.int32, (SLAB, 128), 0) + plan["off_r"]
             from_r = (row >= 0) & (row < plan["got_q"])
-            for k in range(PER * j, PER * (j + 1)):
+            for k in range(first, end):
                 frame_x[k, X_BASE : X_BASE + SLAB] = jnp.where(
                     from_r,
                     frame_r[k, pl.ds(FR_BASE + plan["off_r"], SLAB), :],
-                    land[3 * p + 1, k],
+                    land[3 * p + 1, SLAB * k : SLAB * (k + 1)],
                 )
 
         def tile(t, carry):
@@ -202,7 +233,7 @@
                 from_x = (row >= plan["xs"]) & (row < plan["xe"])
             if last:
                 full = row < plan["count"]
-            for k in range(PER * j, PER * (j + 1)):
+            for k in range(first, end):
                 value = jnp.where(
                     from_p,
                     frame_p[k, pl.ds(FP_BASE - plan["fs"] + base, 8), :],
@@ -213,23 +244,44 @@
                         from_x, frame_x[k, pl.ds(X_BASE - plan["xs"] + base, 8), :], value
                     )
                 if last:
-                    final[k, pl.ds(base, 8), :] = jnp.where(full, value, -1.0 if k == 7 else 0.0)
+                    final[k, pl.ds(base, 8), :] = jnp.where(full, value, 0.0)
                 else:
                     lists[(p + 1) % 2][k, pl.ds(LIST_BASE + base, 8), :] = value
             return carry
 
         lax.fori_loop(0, CAP // 8, tile, 0, unroll=True)
-
+        if end == COMPS:
+            lane = lax.broadcasted_iota(jnp.int32, (8, 128), 1)
+            value = jnp.where(
+                (lane >= plan["fs"]) & (lane < plan["fe"]),
+                to_left(land[3 * p, LEAF_ROWS], -plan["fs"]),
+                to_left(leaf_list[p], plan["list_off"]),
+            )
+            if two:
+                at = lane + plan["off_r"]
+                second = jnp.where(
+                    (at >= 0) & (at < plan["got_q"]),
+                    to_left(land[3 * p + 2, LEAF_ROWS], plan["off_r"]),
+                    land[3 * p + 1, LEAF_ROWS],
+                )
+                value = jnp.where(
+                    (lane >= plan["xs"]) & (lane < plan["xe"]), to_left(second, -plan["xs"]), value
+                )
+            if last:
+                leaf_final[...] = jnp.where(lane < plan["count"], value, -1.0).astype(jnp.int32)
+            else:
+                leaf_list[p + 1] = value
+
+    for load in loads[2:]:
+        load.wait()
+    leaf_list[0] = jnp.broadcast_to(leaves[...], (8, 128)).astype(jnp.float32)
     pl.semaphore_wait(barrier, partners)
-    for j in range(CHUNKS):
+    for j in range(len(CHUNKS)):
         send(0, j)
-    for t in range(len(PHASES) + CHUNKS - 1):
-        for j in reversed(range(CHUNKS)):
-            p = t - j
-            if 0 <= p < len(PHASES):
-                receive(p, j)
-                if p + 1 < len(PHASES):
-                    send(p + 1, j)
+    for p, j in ORDER_OF_WORK:
+        receive(p, j)
+        if p + 1 < len(PHASES):
+            send(p + 1, j)
     for copies in started.values():
         for copy in copies:
             copy.wait_send()
@@ -258,7 +310,7 @@
     return jnp.dot(left, right, preferred_element_type=jnp.float32)
 
 
-def moments(final, table, positions, charges, velocities, leaves, leaf_out, parent_out,
+def moments(final, leaf_final, table, positions, charges, velocities, leaves, leaf_out, parent_out,
             u_ref, v_ref, w_ref, a_ref, b_ref, flip_ref, sign_ref, copy_sem):
     copies = [
         pltpu.make_async_copy(final.at[0:3], positions, copy_sem.at[0]),
@@ -267,8 +319,7 @@
     ]
     for copy in copies:
         copy.start()
-    leaf_rows = final[7]
-    leaf_row = leaf_rows.T[0:8].astype(jnp.int32)
+    leaf_row = leaf_final[...]
     leaves[...] = leaf_row[0:1]
     live_row = leaf_row >= 0
     leaf = jnp.where(live_row, leaf_row, 0)
@@ -328,7 +379,7 @@
     matrix = table[...]
     shifted = (dot32(matrix, low) + dot32(matrix, middle)) + dot32(matrix, high)
     shifted = shifted * sign_ref[...]
-    leaf_col = leaf_rows.astype(jnp.int32)
+    leaf_col = jnp.broadcast_to(leaf_row[0:1].astype(jnp.float32), (CAP, 128)).T.astype(jnp.int32)
     sibling = (
         ((leaf_col >> 3) == (leaf_row >> 3)[0:1]) & (leaf_col >= 0) & live_row[0:1]
     ).astype(jnp.float32).astype(jnp.bfloat16)
@@ -344,28 +395,35 @@
     smem = pl.BlockSpec(memory_space=pltpu.SMEM)
     anywhere = pl.BlockSpec(memory_space=pl.ANY)
     f32 = jnp.float32
-    copies = len(FRAMES) * CHUNKS
-    final = pl.pallas_call(
+    copies = len(FRAMES) * len(CHUNKS)
+    final, leaf_final = pl.pallas_call(
         exchange,
         name="exchange",
-        out_shape=jax.ShapeDtypeStruct((COMPS, CAP, 128), f32),
-        in_specs=[smem, smem, vmem, vmem, vmem, vmem],
-        out_specs=vmem,
+        out_shape=(
+            jax.ShapeDtypeStruct((COMPS, CAP, 128), f32),
+            jax.ShapeDtypeStruct((8, CAP), jnp.int32),
+        ),
+        in_specs=[anywhere] * 6,
+        out_specs=(vmem, vmem),
         scratch_shapes=[
+            pltpu.SMEM((256,), jnp.int32),
+            pltpu.SMEM((8, 256), jnp.int32),
+            pltpu.VMEM((1, CAP), jnp.int32),
             pltpu.VMEM((COMPS, LIST_BASE + CAP + 64, 128), f32),
             pltpu.VMEM((COMPS, LIST_BASE + CAP + 64, 128), f32),
             pltpu.VMEM((COMPS, FP_BASE + CAP + 64, 128), f32),
             pltpu.VMEM((COMPS, FR_BASE + 2 * SLAB, 128), f32),
             pltpu.VMEM((COMPS, X_BASE + CAP, 128), f32),
-            pltpu.VMEM((2 * len(PHASES), COMPS, SLAB, 128), f32),
-            pltpu.VMEM((3 * len(PHASES), COMPS, SLAB, 128), f32),
+            pltpu.VMEM((2 * len(PHASES), FRAME, 128), f32),
+            pltpu.VMEM((3 * len(PHASES), FRAME, 128), f32),
+            pltpu.SemaphoreType.DMA((3 + COMPS,)),
             pltpu.SemaphoreType.DMA((copies,)),
             pltpu.SemaphoreType.DMA((copies,)),
         ],
         compiler_params=pltpu.CompilerParams(
-            collective_id=0, has_side_effects=True, vmem_limit_bytes=24 * 2**20
+            collective_id=0, has_side_effects=True, vmem_limit_bytes=VMEM_LIMIT
         ),
-    )(live_counts, send_counts, leaf_ids.reshape(1, CAP), positions, charges, velocities)
+    )(*(pltpu.with_memory_space_constraint(x, pltpu.HBM) for x in (live_counts, send_counts, leaf_ids.reshape(1, CAP), positions, charges, velocities)))
 
     square = pltpu.VMEM((CAP, 128), f32)
     outs = pl.pallas_call(
@@ -379,7 +437,7 @@
             jax.ShapeDtypeStruct((NCOEF, CAP), f32),
             jax.ShapeDtypeStruct((NCOEF, CAP), f32),
         ),
-        in_specs=[vmem, vmem],
+        in_specs=[vmem, vmem, vmem],
         out_specs=(anywhere, anywhere, anywhere, vmem, vmem, vmem),
         scratch_shapes=[square] * 5
         + [
@@ -388,7 +446,7 @@
             pltpu.SemaphoreType.DMA((3,)),
         ],
         compiler_params=pltpu.CompilerParams(vmem_limit_bytes=16 * 2**20),
-    )(final, shift_table())
+    )(final, leaf_final, shift_table())
     moved_positions, moved_charges, moved_velocities, moved_leaves, leaf_part, parent_part = outs
     return (
         moved_positions,

time: 50.1 us -> 41.8 us (0.83)
  Pallas kernels: 45.2 us -> 41 us
  local copies, waits for them, and re-layouts: 4.06 us -> 0.01 us
    pallas_call x1, Pallas kernels: 41 us -> 37 us  [per_device(): pl.pallas_call(exchange, name='exchange', out_shape=(jax.ShapeDtypeStruct...]
    unnamed x14 -> x2, local copies, waits for them, and re-layouts: 4.06 us -> 0.01 us
where the time goes in v1:
time: 41.8 us; the launch traced here: 41.7 us
  Pallas kernels  41 us (98%)
  between operations  0.66 us (2%)
    pallas_call x1, Pallas kernels, per_device(): pl.pallas_call(exchange, name='exchange', out_shape=(jax.ShapeDtypeStruct...  37 us
    pallas_call x1, Pallas kernels, per_device(): pl.pallas_call(moments, name='moments', out_shape=(jax.ShapeDtypeStruct((...  4.06 us

profile of v1, /device:TPU:1, one launch (start us, length us, event | category | flops | bytes accessed | tf_op | source)
XLA Modules:
  0.0 41.7 jit_solution(17001879509209327582)
XLA Ops:
  0.6 0.0 copy-start
  0.6 37.0 %exchange.1 = (f32[7,128,128]{2,1,0:T(8,128)S(1)}, s32[8,128]{1,0:T(8,128)S(1)}) custom-call(s32[256]{0:T(256)} %live_hbm.1, s32[8,256]{1,0:T(8,128)} %sends_hbm.1, s32[1,128]{1,0:T(1,128)} %bitcast.2, f32[3,128,128]{2,1,0:T(8,128)} %positions.1, f32[128,128]{1,0:T(8,128)} %charges.1, f32[3,128,128]{2,1,0:T(8,128)} %velocities.1), custom_call_target="tpu_custom_call" | custom-call | tf_op jit(solution)/shard_map/exchange/pallas_call | solution.py:399
  37.6 0.0 copy-done
  37.6 4.1 %moments.1 = (f32[3,128,128]{2,1,0:T(8,128)}, f32[128,128]{1,0:T(8,128)}, f32[3,128,128]{2,1,0:T(8,128)}, s32[1,128]{1,0:T(1,128)}, f32[286,128]{1,0:T(8,128)}, /*index=5*/f32[286,128]{1,0:T(8,128)}) custom-call(f32[7,128,128]{2,1,0:T(8,128)S(1)} %get-tuple-element.14.final, s32[8,128]{1,0:T(8,128)S(1)} %get-tuple-element.15.leaf_final, ...), custom_call_target="tpu_custom_call" | custom-call | tf_op jit(solution)/shard_map/moments/pallas_call | solution.py:429
Async XLA Ops:
  0.6 37.0 %copy-start = (bf16[288,288]{1,0:T(8,128)(2,1)S(1)}, bf16[288,288]{1,0:T(8,128)(2,1)}, u32[]{:S(2)}) copy-start(bf16[288,288]{1,0:T(8,128)(2,1)} %constant.2.clone.table) | copy-start | bytes 497668

commit v2 on v1

--- a/solution.py
+++ b/solution.py
@@ -15,8 +15,8 @@
 SLAB = 32
 COMPS = 7
 FRAME = SLAB * COMPS + 8
-LEAF_ROWS = slice(SLAB * COMPS, FRAME)
-CHUNKS = ((0, 2), (2, 5), (5, 7))
+LEAF_ROWS = slice(SLAB * 4, SLAB * 4 + 8)
+CHUNKS = ((0, 1), (1, 2), (2, 4), (4, 6), (6, 7))
 MESH = pl.DeviceIdType.MESH
 
 PHASES = (
@@ -30,12 +30,11 @@
 STRIDES = {"gx": 64, "gy": 8, "gz": 1}
 FRAMES = [(p, slot) for p, phase in enumerate(PHASES) for slot in range(2 ** len(phase[1]) - 1)]
 VMEM_LIMIT = 24 * 2**20
-ORDER_OF_WORK = [
-    (t - j, j)
-    for t in range(len(PHASES) + len(CHUNKS) - 1)
-    for j in reversed(range(len(CHUNKS)))
-    if 0 <= t - j < len(PHASES)
-]
+ORDER_OF_WORK = (
+    [(0, 0), (0, 1), (0, 2), (0, 3), (0, 4), (1, 0), (1, 1), (2, 0), (2, 1), (1, 2), (1, 3), (2, 2)]
+    + [(1, 4), (2, 3), (2, 4), (3, 0), (3, 1), (3, 2), (4, 0), (4, 1), (3, 3), (4, 2), 0, (3, 4), 1]
+    + [2, 3, (4, 3), (4, 4)]
+)
 LIST_BASE = 64
 FP_BASE = 160
 X_BASE = 128
@@ -58,13 +57,25 @@
     return {4: high, 2: middle, 1: rest - 2 * middle}
 
 
+def rows_of(first, end):
+    return slice(SLAB * first + 8 * (first >= 4), SLAB * end + 8 * (end >= 4))
+
+
+def frame_rows(k):
+    start = SLAB * k + 8 * (k >= 4)
+    return slice(start, start + SLAB)
+
+
 def pick(bit, one, zero):
     return bit * one + (1 - bit) * zero
 
 
-def exchange(live_hbm, sends_hbm, leaves_hbm, positions, charges, velocities, final, leaf_final,
+def exchange(live_hbm, sends_hbm, leaves_hbm, positions, charges, velocities, table_hbm,
+             final, leaf_final, leaf_out, parent_out,
              live, sends, leaves, list_a, list_b, frame_p, frame_r, frame_x, out, land,
-             load_sem, send_sem, recv_sem):
+             table, u_ref, v_ref, w_ref, a_ref, b_ref, flip_ref, sign_ref,
+             load_sem, send_sem, recv_sem, vouched):
+    moment_refs = (leaf_out, parent_out, u_ref, v_ref, w_ref, a_ref, b_ref, flip_ref, sign_ref)
     where = {axis: lax.axis_index(axis) for axis in SIZES}
     bits = {axis: bits_of(where[axis]) for axis in SIZES}
     me = sum(where[axis] * STRIDES[axis] for axis in SIZES)
@@ -85,6 +96,8 @@
     partners = 0
     for axis, masks, _ in PHASES:
         for mask in masks + ((sum(masks),) if len(masks) == 2 else ()):
+            if (axis, mask) == ("gz", 4):
+                continue
             pl.semaphore_signal(
                 barrier, inc=1, device_id=peer(axis, mask), device_id_type=MESH
             )
@@ -95,6 +108,7 @@
     pairs += [(positions.at[k], list_a.at[k, body]) for k in range(3)]
     pairs += [(charges, list_a.at[3, body])]
     pairs += [(velocities.at[k], list_a.at[4 + k, body]) for k in range(3)]
+    pairs += [(table_hbm, table)]
     loads = [
         pltpu.make_async_copy(source, target, load_sem.at[k])
         for k, (source, target) in enumerate(pairs)
@@ -161,7 +175,7 @@
     def transfers(p, j):
         axis, masks, _ = PHASES[p]
         first, end = CHUNKS[j]
-        rows = slice(SLAB * first, SLAB * end + (8 if end == COMPS else 0))
+        rows = rows_of(first, end)
         todo = [(0, 0, masks[0])]
         if len(masks) == 2:
             todo += [(1, 1, masks[1]), (2, 0, masks[0] + masks[1])]
@@ -191,11 +205,11 @@
         first, end = CHUNKS[j]
         two = "start_q" in plan
         for k in range(first, end):
-            rows = slice(SLAB * k, SLAB * (k + 1))
+            rows = frame_rows(k)
             out[2 * p, rows] = now[k, pl.ds(LIST_BASE + plan["start_a"], SLAB), :]
             if two:
                 out[2 * p + 1, rows] = now[k, pl.ds(LIST_BASE + plan["start_q"], SLAB), :]
-        if end == COMPS:
+        if end == 4:
             out[2 * p, LEAF_ROWS] = to_left(leaf_list[p], plan["start_a"])
             if two:
                 out[2 * p + 1, LEAF_ROWS] = to_left(leaf_list[p], plan["start_q"])
@@ -211,7 +225,7 @@
             copy.wait_recv()
         two = "start_q" in plan
         for k in range(first, end):
-            rows = slice(SLAB * k, SLAB * (k + 1))
+            rows = frame_rows(k)
             frame_p[k, FP_BASE : FP_BASE + SLAB] = land[3 * p, rows]
             if two:
                 frame_r[k, FR_BASE : FR_BASE + SLAB] = land[3 * p + 2, rows]
@@ -222,7 +236,7 @@
                 frame_x[k, X_BASE : X_BASE + SLAB] = jnp.where(
                     from_r,
                     frame_r[k, pl.ds(FR_BASE + plan["off_r"], SLAB), :],
-                    land[3 * p + 1, SLAB * k : SLAB * (k + 1)],
+                    land[3 * p + 1, frame_rows(k)],
                 )
 
         def tile(t, carry):
@@ -250,7 +264,7 @@
             return carry
 
         lax.fori_loop(0, CAP // 8, tile, 0, unroll=True)
-        if end == COMPS:
+        if end == 4:
             lane = lax.broadcasted_iota(jnp.int32, (8, 128), 1)
             value = jnp.where(
                 (lane >= plan["fs"]) & (lane < plan["fe"]),
@@ -278,9 +292,17 @@
     pl.semaphore_wait(barrier, partners)
     for j in range(len(CHUNKS)):
         send(0, j)
-    for p, j in ORDER_OF_WORK:
+    pl.semaphore_signal(vouched, inc=1, device_id=peer("gz", 6), device_id_type=MESH)
+    moments = moment_pieces(final, leaf_final, table, *moment_refs)
+    for work in ORDER_OF_WORK:
+        if isinstance(work, int):
+            moments[work]()
+            continue
+        p, j = work
         receive(p, j)
         if p + 1 < len(PHASES):
+            if (p + 1, j) == (3, 0):
+                pl.semaphore_wait(vouched, 1)
             send(p + 1, j)
     for copies in started.values():
         for copy in copies:
@@ -310,82 +332,127 @@
     return jnp.dot(left, right, preferred_element_type=jnp.float32)
 
 
-def moments(final, leaf_final, table, positions, charges, velocities, leaves, leaf_out, parent_out,
-            u_ref, v_ref, w_ref, a_ref, b_ref, flip_ref, sign_ref, copy_sem):
-    copies = [
-        pltpu.make_async_copy(final.at[0:3], positions, copy_sem.at[0]),
-        pltpu.make_async_copy(final.at[3], charges, copy_sem.at[1]),
-        pltpu.make_async_copy(final.at[4:7], velocities, copy_sem.at[2]),
+def packed_sums(parts):
+    row = lax.broadcasted_iota(jnp.int32, (8, 128), 0)
+    low = row < 4
+    parts = [
+        jnp.where(low, one, two) + pltpu.roll(jnp.where(low, two, one), 4, 0)
+        for one, two in zip(parts[:4], parts[4:])
     ]
+    for half in (2, 1):
+        low = row % (2 * half) < half
+        parts = [
+            jnp.where(low, one, two)
+            + jnp.where(low, pltpu.roll(one, 8 - half, 0), pltpu.roll(two, half, 0))
+            for one, two in zip(parts[:half], parts[half:])
+        ]
+    return parts[0]
+
+
+def moment_pieces(final, leaf_final, table, leaf_out, parent_out,
+                  u_ref, v_ref, w_ref, a_ref, b_ref, flip_ref, sign_ref):
+    state = {"sums": [], "k": 0}
+    step = 8
+
+    def begin():
+        leaf_row = leaf_final[...]
+        leaf = jnp.where(leaf_row >= 0, leaf_row, 0)
+        cells = []
+        for axis_bit in (2, 1, 0):
+            cell = jnp.zeros_like(leaf)
+            for level in range(LEVEL):
+                cell = cell + ((leaf >> (3 * level + axis_bit)) & 1) * 2**level
+            cells.append(cell[0:1].astype(jnp.float32))
+        for axis, ref in enumerate((u_ref, v_ref, w_ref)):
+            ref[...] = 2.0 * (final[axis].T * float(2**LEVEL) - cells[axis]) - 1.0
+        a_ref[...] = final[3].T * (1.0 / 16.0)
+        state["flips"] = [
+            jnp.where(((leaf >> bit) & 1) == 1, 1.0, -1.0).astype(jnp.float32) for bit in (2, 1, 0)
+        ]
+
+    def store(parts, first):
+        parts = parts + [jnp.zeros((8, 128), jnp.float32)] * (8 - len(parts))
+        rows = packed_sums(parts)
+        row = lax.broadcasted_iota(jnp.int32, (8, 128), 0)
+        sign = jnp.ones((8, 128), jnp.float32)
+        for axis in range(3):
+            odd = sum(
+                (TRIPLES[first + i][axis] & 1) << i for i in range(8) if first + i < NCOEF
+            )
+            if odd:
+                sign = sign * jnp.where((odd >> row) & 1 == 1, state["flips"][axis], 1.0)
+        count = min(8, NCOEF - first)
+        leaf_out[first : first + count] = rows[:count]
+        flip_ref[first : first + 8] = rows * sign
+        sign_ref[first : first + 8] = sign
+
+    def sums_of(orders):
+        for p in orders:
+            for q in range(ORDER + 1 - p):
+                count = ORDER + 1 - p - q
+
+                def body(g, sums, first=q == 0, more_q=q < ORDER - p, more_p=p < ORDER, count=count):
+                    sums = list(sums)
+                    for i in range(step):
+                        rows = pl.ds((g * step + i) * 8, 8)
+                        term = (a_ref if first else b_ref)[rows, :]
+                        if more_q:
+                            b_ref[rows, :] = term * v_ref[rows, :]
+                        if first and more_p:
+                            a_ref[rows, :] = term * u_ref[rows, :]
+                        w = w_ref[rows, :]
+                        for r in range(count):
+                            sums[r] = sums[r] + term
+                            if r + 1 < count:
+                                term = term * w
+                    return tuple(sums)
+
+                zero = jnp.zeros((8, 128), jnp.float32)
+                state["sums"] += list(lax.fori_loop(0, 16 // step, body, (zero,) * count))
+                while len(state["sums"]) >= 8:
+                    store(state["sums"][:8], state["k"])
+                    state["sums"] = state["sums"][8:]
+                    state["k"] += 8
+        if orders[-1] == ORDER:
+            store(state["sums"], state["k"])
+
+    def parents():
+        high, middle, low = split3(flip_ref[...])
+        matrix = table[...]
+        shifted = (dot32(matrix, low) + dot32(matrix, middle)) + dot32(matrix, high)
+        shifted = shifted * sign_ref[...]
+        leaf_row = leaf_final[0:1]
+        leaf_col = (
+            jnp.broadcast_to(leaf_row.astype(jnp.float32), (CAP, 128)).T.astype(jnp.int32)
+        )
+        sibling = (
+            ((leaf_col >> 3) == (leaf_row >> 3)) & (leaf_col >= 0) & (leaf_row >= 0)
+        ).astype(jnp.float32).astype(jnp.bfloat16)
+        high, middle, low = split3(shifted)
+        total = (dot32(low, sibling) + dot32(middle, sibling)) + dot32(high, sibling)
+        parent_out[...] = total[:NCOEF]
+
+    return (
+        lambda: (begin(), sums_of((0,))),
+        lambda: sums_of((1, 2)),
+        lambda: sums_of(tuple(range(3, ORDER + 1))),
+        parents,
+    )
+
+
+def store_all(final, leaf_final, leaf_in, parent_in, positions, charges, velocities, leaves,
+              leaf_out, parent_out, sem):
+    pairs = (
+        (final.at[0:3], positions),
+        (final.at[3], charges),
+        (final.at[4:7], velocities),
+        (leaf_final.at[0:1], leaves),
+        (leaf_in, leaf_out),
+        (parent_in, parent_out),
+    )
+    copies = [pltpu.make_async_copy(*pair, sem.at[k]) for k, pair in enumerate(pairs)]
     for copy in copies:
         copy.start()
-    leaf_row = leaf_final[...]
-    leaves[...] = leaf_row[0:1]
-    live_row = leaf_row >= 0
-    leaf = jnp.where(live_row, leaf_row, 0)
-    cells = []
-    for axis_bit in (2, 1, 0):
-        cell = jnp.zeros_like(leaf)
-        for level in range(LEVEL):
-            cell = cell + ((leaf >> (3 * level + axis_bit)) & 1) * 2**level
-        cells.append(cell[0:1].astype(jnp.float32))
-    for axis, ref in enumerate((u_ref, v_ref, w_ref)):
-        ref[...] = 2.0 * (final[axis].T * float(2**LEVEL) - cells[axis]) - 1.0
-    a_ref[...] = final[3].T * (1.0 / 16.0)
-    flips = [
-        jnp.where(((leaf >> bit) & 1)[0:1] == 1, 1.0, -1.0).astype(jnp.float32) for bit in (2, 1, 0)
-    ]
-    signs = {}
-    for code in range(8):
-        sign = jnp.ones((1, 128), jnp.float32)
-        for axis in range(3):
-            if code >> (2 - axis) & 1:
-                sign = sign * flips[axis]
-        signs[code] = sign
-    flip_ref[280:288] = jnp.zeros((8, 128), jnp.float32)
-    sign_ref[280:288] = jnp.zeros((8, 128), jnp.float32)
-    step = 8
-    k = 0
-    for p in range(ORDER + 1):
-        for q in range(ORDER + 1 - p):
-            count = ORDER + 1 - p - q
-
-            def body(g, sums, first=q == 0, more_q=q < ORDER - p, more_p=p < ORDER, count=count):
-                sums = list(sums)
-                for i in range(step):
-                    rows = pl.ds((g * step + i) * 8, 8)
-                    term = (a_ref if first else b_ref)[rows, :]
-                    if more_q:
-                        b_ref[rows, :] = term * v_ref[rows, :]
-                    if first and more_p:
-                        a_ref[rows, :] = term * u_ref[rows, :]
-                    w = w_ref[rows, :]
-                    for r in range(count):
-                        sums[r] = sums[r] + term
-                        if r + 1 < count:
-                            term = term * w
-                return tuple(sums)
-
-            zero = jnp.zeros((8, 128), jnp.float32)
-            sums = lax.fori_loop(0, 16 // step, body, (zero,) * count)
-            for r in range(count):
-                row = jnp.sum(sums[r], axis=0, keepdims=True)
-                leaf_out[k : k + 1] = row
-                sign = signs[(p & 1) << 2 | (q & 1) << 1 | (r & 1)]
-                flip_ref[k : k + 1] = row * sign
-                sign_ref[k : k + 1] = sign
-                k += 1
-    high, middle, low = split3(flip_ref[...])
-    matrix = table[...]
-    shifted = (dot32(matrix, low) + dot32(matrix, middle)) + dot32(matrix, high)
-    shifted = shifted * sign_ref[...]
-    leaf_col = jnp.broadcast_to(leaf_row[0:1].astype(jnp.float32), (CAP, 128)).T.astype(jnp.int32)
-    sibling = (
-        ((leaf_col >> 3) == (leaf_row >> 3)[0:1]) & (leaf_col >= 0) & live_row[0:1]
-    ).astype(jnp.float32).astype(jnp.bfloat16)
-    high, middle, low = split3(shifted)
-    total = (dot32(low, sibling) + dot32(middle, sibling)) + dot32(high, sibling)
-    parent_out[...] = total[:NCOEF]
     for copy in copies:
         copy.wait()
 
@@ -396,15 +463,27 @@
     anywhere = pl.BlockSpec(memory_space=pl.ANY)
     f32 = jnp.float32
     copies = len(FRAMES) * len(CHUNKS)
-    final, leaf_final = pl.pallas_call(
+    square = pltpu.VMEM((CAP, 128), f32)
+    operands = (
+        live_counts,
+        send_counts,
+        leaf_ids.reshape(1, CAP),
+        positions,
+        charges,
+        velocities,
+        shift_table(),
+    )
+    results = pl.pallas_call(
         exchange,
         name="exchange",
         out_shape=(
             jax.ShapeDtypeStruct((COMPS, CAP, 128), f32),
             jax.ShapeDtypeStruct((8, CAP), jnp.int32),
+            jax.ShapeDtypeStruct((NCOEF, CAP), f32),
+            jax.ShapeDtypeStruct((NCOEF, CAP), f32),
         ),
-        in_specs=[anywhere] * 6,
-        out_specs=(vmem, vmem),
+        in_specs=[anywhere] * 7,
+        out_specs=(vmem,) * 4,
         scratch_shapes=[
             pltpu.SMEM((256,), jnp.int32),
             pltpu.SMEM((8, 256), jnp.int32),
@@ -416,19 +495,25 @@
             pltpu.VMEM((COMPS, X_BASE + CAP, 128), f32),
             pltpu.VMEM((2 * len(PHASES), FRAME, 128), f32),
             pltpu.VMEM((3 * len(PHASES), FRAME, 128), f32),
-            pltpu.SemaphoreType.DMA((3 + COMPS,)),
+            pltpu.VMEM((ROWS, ROWS), jnp.bfloat16),
+        ]
+        + [square] * 5
+        + [
+            pltpu.VMEM((ROWS, 128), f32),
+            pltpu.VMEM((ROWS, 128), f32),
+            pltpu.SemaphoreType.DMA((4 + COMPS,)),
             pltpu.SemaphoreType.DMA((copies,)),
             pltpu.SemaphoreType.DMA((copies,)),
+            pltpu.SemaphoreType.REGULAR,
         ],
         compiler_params=pltpu.CompilerParams(
             collective_id=0, has_side_effects=True, vmem_limit_bytes=VMEM_LIMIT
         ),
-    )(*(pltpu.with_memory_space_constraint(x, pltpu.HBM) for x in (live_counts, send_counts, leaf_ids.reshape(1, CAP), positions, charges, velocities)))
-
-    square = pltpu.VMEM((CAP, 128), f32)
+    )(*(pltpu.with_memory_space_constraint(operand, pltpu.HBM) for operand in operands))
+
     outs = pl.pallas_call(
-        moments,
-        name="moments",
+        store_all,
+        name="store_all",
         out_shape=(
             jax.ShapeDtypeStruct((3, CAP, 128), f32),
             jax.ShapeDtypeStruct((CAP, 128), f32),
@@ -437,16 +522,11 @@
             jax.ShapeDtypeStruct((NCOEF, CAP), f32),
             jax.ShapeDtypeStruct((NCOEF, CAP), f32),
         ),
-        in_specs=[vmem, vmem, vmem],
-        out_specs=(anywhere, anywhere, anywhere, vmem, vmem, vmem),
-        scratch_shapes=[square] * 5
-        + [
-            pltpu.VMEM((ROWS, 128), f32),
-            pltpu.VMEM((ROWS, 128), f32),
-            pltpu.SemaphoreType.DMA((3,)),
-        ],
-        compiler_params=pltpu.CompilerParams(vmem_limit_bytes=16 * 2**20),
-    )(final, leaf_final, shift_table())
+        in_specs=[vmem] * 4,
+        out_specs=(anywhere,) * 6,
+        scratch_shapes=[pltpu.SemaphoreType.DMA((6,))],
+        compiler_params=pltpu.CompilerParams(vmem_limit_bytes=4 * 2**20),
+    )(*results)
     moved_positions, moved_charges, moved_velocities, moved_leaves, leaf_part, parent_part = outs
     return (
         moved_positions,

time: 41.8 us -> 39.1 us (0.935)
  Pallas kernels: 41 us -> 38.4 us
    pallas_call x1, Pallas kernels: 4.06 us -> 0.92 us  [per_device(): pl.pallas_call(store_all, name='store_all', out_shape=(jax.ShapeDtypeStru...]
    pallas_call x1, Pallas kernels: 37 us -> 37.4 us  [per_device(): pl.pallas_call(exchange, name='exchange', out_shape=(jax.ShapeDtypeStruct...]
where the time goes in v2:
time: 39.1 us; the launch traced here: 39 us
  Pallas kernels  38.4 us (98%)
  between operations  0.64 us (2%)
    pallas_call x1, Pallas kernels, per_device(): pl.pallas_call(exchange, name='exchange', out_shape=(jax.ShapeDtypeStruct...  37.4 us
    pallas_call x1, Pallas kernels, per_device(): pl.pallas_call(store_all, name='store_all', out_shape=(jax.ShapeDtypeStru...  0.92 us

profile of v2, /device:TPU:1, one launch (start us, length us, event | category | flops | bytes accessed | tf_op | source)
XLA Modules:
  0.0 39.0 jit_solution(17329358465289704408)
XLA Ops:
  0.6 37.4 %exchange.1 = (f32[7,128,128]{2,1,0:T(8,128)S(1)}, s32[8,128]{1,0:T(8,128)S(1)}, f32[286,128]{1,0:T(8,128)S(1)}, f32[286,128]{1,0:T(8,128)S(1)}) custom-call(s32[256]{0:T(256)} %live_hbm.1, s32[8,256]{1,0:T(8,128)} %sends_hbm.1, s32[1,128]{1,0:T(1,128)} %bitcast.2, f32[3,128,128]{2,1,0:T(8,128)} %positions.1, f32[128,128]{1,0:T(8,128)} %charges.1, ...), custom_call_target="tpu_custom_call" | custom-call | tf_op jit(solution)/shard_map/exchange/pallas_call | solution.py:476
  38.1 0.9 %store_all.1 = (f32[3,128,128]{2,1,0:T(8,128)}, f32[128,128]{1,0:T(8,128)}, f32[3,128,128]{2,1,0:T(8,128)}, s32[1,128]{1,0:T(1,128)}, f32[286,128]{1,0:T(8,128)}, /*index=5*/f32[286,128]{1,0:T(8,128)}) custom-call(f32[7,128,128]{2,1,0:T(8,128)S(1)} %get-tuple-element.16.final, s32[8,128]{1,0:T(8,128)S(1)} %get-tuple-element.17.leaf_final, ...), custom_call_target="tpu_custom_call" | custom-call | tf_op jit(solution)/shard_map/store_all/pallas_call | solution.py:514

commit v3 on v2

--- a/solution.py
+++ b/solution.py
@@ -20,21 +20,17 @@
 MESH = pl.DeviceIdType.MESH
 
 PHASES = (
-    ("gx", (2, 1), 0),
-    ("gy", (4, 2), 2),
-    ("gy", (1,), 4),
-    ("gz", (4, 2), 5),
-    ("gz", (1,), 7),
+('gx', (2, 1), 0),
+('gy', (4, 2), 2),
+('gy', (1,), 4),
+('gz', (4, 2), 5),
+('gz', (1,), 7),
 )
 SIZES = {"gx": 4, "gy": 8, "gz": 8}
 STRIDES = {"gx": 64, "gy": 8, "gz": 1}
 FRAMES = [(p, slot) for p, phase in enumerate(PHASES) for slot in range(2 ** len(phase[1]) - 1)]
 VMEM_LIMIT = 24 * 2**20
-ORDER_OF_WORK = (
-    [(0, 0), (0, 1), (0, 2), (0, 3), (0, 4), (1, 0), (1, 1), (2, 0), (2, 1), (1, 2), (1, 3), (2, 2)]
-    + [(1, 4), (2, 3), (2, 4), (3, 0), (3, 1), (3, 2), (4, 0), (4, 1), (3, 3), (4, 2), 0, (3, 4), 1]
-    + [2, 3, (4, 3), (4, 4)]
-)
+ORDER_OF_WORK = [(-1, 0), (-1, 1), (-1, 2), (-1, 3), (-1, 4), (0, 0), (0, 1), (0, 2), (1, 0), (0, 3), (1, 1), (2, 0), (0, 4), (2, 1), (1, 2), (2, 2), (1, 3), (1, 4), (2, 3), (3, 0), (2, 4), (3, 1), (3, 2), (4, 0), (3, 3), (4, 1), (4, 2), 0, (3, 4), 1, 2, 3, (4, 3), (4, 4)]
 LIST_BASE = 64
 FP_BASE = 160
 X_BASE = 128
@@ -290,8 +286,6 @@
         load.wait()
     leaf_list[0] = jnp.broadcast_to(leaves[...], (8, 128)).astype(jnp.float32)
     pl.semaphore_wait(barrier, partners)
-    for j in range(len(CHUNKS)):
-        send(0, j)
     pl.semaphore_signal(vouched, inc=1, device_id=peer("gz", 6), device_id_type=MESH)
     moments = moment_pieces(final, leaf_final, table, *moment_refs)
     for work in ORDER_OF_WORK:
@@ -299,7 +293,8 @@
             moments[work]()
             continue
         p, j = work
-        receive(p, j)
+        if p >= 0:
+            receive(p, j)
         if p + 1 < len(PHASES):
             if (p + 1, j) == (3, 0):
                 pl.semaphore_wait(vouched, 1)
@@ -352,7 +347,7 @@
 def moment_pieces(final, leaf_final, table, leaf_out, parent_out,
                   u_ref, v_ref, w_ref, a_ref, b_ref, flip_ref, sign_ref):
     state = {"sums": [], "k": 0}
-    step = 8
+    step = 16
 
     def begin():
         leaf_row = leaf_final[...]

time: 39.1 us -> 38.1 us (0.974)
  Pallas kernels: 38.4 us -> 37.4 us
    pallas_call x1, Pallas kernels: 37.4 us -> 36.5 us  [per_device(): pl.pallas_call(exchange, name='exchange', out_shape=(jax.ShapeDtypeStruct...]
where the time goes in v3:
time: 38.1 us; the launch traced here: 38 us
  Pallas kernels  37.4 us (98%)
  between operations  0.64 us (2%)
    pallas_call x1, Pallas kernels, per_device(): pl.pallas_call(exchange, name='exchange', out_shape=(jax.ShapeDtypeStruct...  36.5 us
    pallas_call x1, Pallas kernels, per_device(): pl.pallas_call(store_all, name='store_all', out_shape=(jax.ShapeDtypeStru...  0.92 us

profile of v3, /device:TPU:1, one launch (start us, length us, event | category | flops | bytes accessed | tf_op | source)
XLA Modules:
  0.0 38.0 jit_solution(6169753274208504579)
XLA Ops:
  0.6 36.5 %exchange.1 = (f32[7,128,128]{2,1,0:T(8,128)S(1)}, s32[8,128]{1,0:T(8,128)S(1)}, f32[286,128]{1,0:T(8,128)S(1)}, f32[286,128]{1,0:T(8,128)S(1)}) custom-call(s32[256]{0:T(256)} %live_hbm.1, s32[8,256]{1,0:T(8,128)} %sends_hbm.1, s32[1,128]{1,0:T(1,128)} %bitcast.2, f32[3,128,128]{2,1,0:T(8,128)} %positions.1, f32[128,128]{1,0:T(8,128)} %charges.1, ...), custom_call_target="tpu_custom_call" | custom-call | tf_op jit(solution)/shard_map/exchange/pallas_call | solution.py:471
  37.1 0.9 %store_all.1 = (f32[3,128,128]{2,1,0:T(8,128)}, f32[128,128]{1,0:T(8,128)}, f32[3,128,128]{2,1,0:T(8,128)}, s32[1,128]{1,0:T(1,128)}, f32[286,128]{1,0:T(8,128)}, /*index=5*/f32[286,128]{1,0:T(8,128)}) custom-call(f32[7,128,128]{2,1,0:T(8,128)S(1)} %get-tuple-element.16.final, s32[8,128]{1,0:T(8,128)S(1)} %get-tuple-element.17.leaf_final, ...), custom_call_target="tpu_custom_call" | custom-call | tf_op jit(solution)/shard_map/store_all/pallas_call | solution.py:509

commit v4 on v3

--- a/solution.py
+++ b/solution.py
@@ -30,7 +30,7 @@
 STRIDES = {"gx": 64, "gy": 8, "gz": 1}
 FRAMES = [(p, slot) for p, phase in enumerate(PHASES) for slot in range(2 ** len(phase[1]) - 1)]
 VMEM_LIMIT = 24 * 2**20
-ORDER_OF_WORK = [(-1, 0), (-1, 1), (-1, 2), (-1, 3), (-1, 4), (0, 0), (0, 1), (0, 2), (1, 0), (0, 3), (1, 1), (2, 0), (0, 4), (2, 1), (1, 2), (2, 2), (1, 3), (1, 4), (2, 3), (3, 0), (2, 4), (3, 1), (3, 2), (4, 0), (3, 3), (4, 1), (4, 2), 0, (3, 4), 1, 2, 3, (4, 3), (4, 4)]
+ORDER_OF_WORK = [(-1, 0), (-1, 1), (-1, 2), (-1, 3), (-1, 4), (0, 0), (0, 1), (0, 2), (1, 0), (0, 3), (1, 1), (2, 0), (0, 4), (2, 1), (1, 2), (2, 2), (1, 3), (1, 4), (2, 3), (3, 0), (2, 4), (3, 1), (3, 2), (4, 0), 5, (3, 3), (4, 1), 6, (3, 4), (4, 2), 0, 1, 2, (4, 3), 3, 4, (4, 4)]
 LIST_BASE = 64
 FP_BASE = 160
 X_BASE = 128
@@ -347,7 +347,12 @@
 def moment_pieces(final, leaf_final, table, leaf_out, parent_out,
                   u_ref, v_ref, w_ref, a_ref, b_ref, flip_ref, sign_ref):
     state = {"sums": [], "k": 0}
-    step = 16
+
+    def turn_x():
+        u_ref[...] = final[0].T
+
+    def turn_y():
+        v_ref[...] = final[1].T
 
     def begin():
         leaf_row = leaf_final[...]
@@ -358,9 +363,10 @@
             for level in range(LEVEL):
                 cell = cell + ((leaf >> (3 * level + axis_bit)) & 1) * 2**level
             cells.append(cell[0:1].astype(jnp.float32))
+        w_ref[...] = final[2].T
+        a_ref[...] = final[3].T * (1.0 / 16.0)
         for axis, ref in enumerate((u_ref, v_ref, w_ref)):
-            ref[...] = 2.0 * (final[axis].T * float(2**LEVEL) - cells[axis]) - 1.0
-        a_ref[...] = final[3].T * (1.0 / 16.0)
+            ref[...] = 2.0 * (ref[...] * float(2**LEVEL) - cells[axis]) - 1.0
         state["flips"] = [
             jnp.where(((leaf >> bit) & 1) == 1, 1.0, -1.0).astype(jnp.float32) for bit in (2, 1, 0)
         ]
@@ -386,24 +392,20 @@
             for q in range(ORDER + 1 - p):
                 count = ORDER + 1 - p - q
 
-                def body(g, sums, first=q == 0, more_q=q < ORDER - p, more_p=p < ORDER, count=count):
-                    sums = list(sums)
-                    for i in range(step):
-                        rows = pl.ds((g * step + i) * 8, 8)
-                        term = (a_ref if first else b_ref)[rows, :]
-                        if more_q:
-                            b_ref[rows, :] = term * v_ref[rows, :]
-                        if first and more_p:
-                            a_ref[rows, :] = term * u_ref[rows, :]
-                        w = w_ref[rows, :]
-                        for r in range(count):
-                            sums[r] = sums[r] + term
-                            if r + 1 < count:
-                                term = term * w
-                    return tuple(sums)
-
-                zero = jnp.zeros((8, 128), jnp.float32)
-                state["sums"] += list(lax.fori_loop(0, 16 // step, body, (zero,) * count))
+                sums = [None] * count
+                for g in range(16):
+                    rows = slice(8 * g, 8 * g + 8)
+                    term = (a_ref if q == 0 else b_ref)[rows, :]
+                    if q < ORDER - p:
+                        b_ref[rows, :] = term * v_ref[rows, :]
+                    if q == 0 and p < ORDER:
+                        a_ref[rows, :] = term * u_ref[rows, :]
+                    w = w_ref[rows, :]
+                    for r in range(count):
+                        sums[r] = term if g == 0 else sums[r] + term
+                        if r + 1 < count:
+                            term = term * w
+                state["sums"] += sums
                 while len(state["sums"]) >= 8:
                     store(state["sums"][:8], state["k"])
                     state["sums"] = state["sums"][8:]
@@ -428,10 +430,13 @@
         parent_out[...] = total[:NCOEF]
 
     return (
-        lambda: (begin(), sums_of((0,))),
+        begin,
+        lambda: sums_of((0,)),
         lambda: sums_of((1, 2)),
         lambda: sums_of(tuple(range(3, ORDER + 1))),
         parents,
+        turn_x,
+        turn_y,
     )
 
 

time: 38.1 us -> 37.6 us (0.987)
  Pallas kernels: 37.4 us -> 36.9 us
    pallas_call x1, Pallas kernels: 36.5 us -> 35.9 us  [per_device(): pl.pallas_call(exchange, name='exchange', out_shape=(jax.ShapeDtypeStruct...]
where the time goes in v4:
time: 37.6 us; the launch traced here: 37.5 us
  Pallas kernels  36.9 us (98%)
  between operations  0.64 us (2%)
    pallas_call x1, Pallas kernels, per_device(): pl.pallas_call(exchange, name='exchange', out_shape=(jax.ShapeDtypeStruct...  35.9 us
    pallas_call x1, Pallas kernels, per_device(): pl.pallas_call(store_all, name='store_all', out_shape=(jax.ShapeDtypeStru...  0.92 us

profile of v4, /device:TPU:1, one launch (start us, length us, event | category | flops | bytes accessed | tf_op | source)
XLA Modules:
  0.0 37.5 jit_solution(18143793517307870910)
XLA Ops:
  0.6 35.9 %exchange.1 = (f32[7,128,128]{2,1,0:T(8,128)S(1)}, s32[8,128]{1,0:T(8,128)S(1)}, f32[286,128]{1,0:T(8,128)S(1)}, f32[286,128]{1,0:T(8,128)S(1)}) custom-call(s32[256]{0:T(256)} %live_hbm.1, s32[8,256]{1,0:T(8,128)} %sends_hbm.1, s32[1,128]{1,0:T(1,128)} %bitcast.2, f32[3,128,128]{2,1,0:T(8,128)} %positions.1, f32[128,128]{1,0:T(8,128)} %charges.1, ...), custom_call_target="tpu_custom_call" | custom-call | tf_op jit(solution)/shard_map/exchange/pallas_call | solution.py:476
  36.6 0.9 %store_all.1 = (f32[3,128,128]{2,1,0:T(8,128)}, f32[128,128]{1,0:T(8,128)}, f32[3,128,128]{2,1,0:T(8,128)}, s32[1,128]{1,0:T(1,128)}, f32[286,128]{1,0:T(8,128)}, /*index=5*/f32[286,128]{1,0:T(8,128)}) custom-call(f32[7,128,128]{2,1,0:T(8,128)S(1)} %get-tuple-element.16.final, s32[8,128]{1,0:T(8,128)S(1)} %get-tuple-element.17.leaf_final, ...), custom_call_target="tpu_custom_call" | custom-call | tf_op jit(solution)/shard_map/store_all/pallas_call | solution.py:514

commit v5 on v4

--- a/solution.py
+++ b/solution.py
@@ -30,7 +30,7 @@
 STRIDES = {"gx": 64, "gy": 8, "gz": 1}
 FRAMES = [(p, slot) for p, phase in enumerate(PHASES) for slot in range(2 ** len(phase[1]) - 1)]
 VMEM_LIMIT = 24 * 2**20
-ORDER_OF_WORK = [(-1, 0), (-1, 1), (-1, 2), (-1, 3), (-1, 4), (0, 0), (0, 1), (0, 2), (1, 0), (0, 3), (1, 1), (2, 0), (0, 4), (2, 1), (1, 2), (2, 2), (1, 3), (1, 4), (2, 3), (3, 0), (2, 4), (3, 1), (3, 2), (4, 0), 5, (3, 3), (4, 1), 6, (3, 4), (4, 2), 0, 1, 2, (4, 3), 3, 4, (4, 4)]
+ORDER_OF_WORK = [(-1, 0), (-1, 1), (-1, 2), (-1, 3), (-1, 4), (0, 0), (0, 1), (0, 2), (1, 0), (0, 3), (1, 1), (2, 0), (0, 4), (2, 1), (1, 2), (2, 2), (1, 3), (1, 4), (2, 3), (3, 0), (2, 4), (3, 1), (3, 2), (3, 3), (4, 0), 5, (4, 1), 6, (3, 4), (4, 2), 0, 1, 2, (4, 3), 3, 4, (4, 4)]
 LIST_BASE = 64
 FP_BASE = 160
 X_BASE = 128
@@ -174,7 +174,7 @@
         rows = rows_of(first, end)
         todo = [(0, 0, masks[0])]
         if len(masks) == 2:
-            todo += [(1, 1, masks[1]), (2, 0, masks[0] + masks[1])]
+            todo += [(2, 0, masks[0] + masks[1]), (1, 1, masks[1])]
         copies = []
         for slot, source, mask in todo:
             at = FRAMES.index((p, slot)) * len(CHUNKS) + j

time: 37.6 us -> 37.6 us (level)
  no operation moved by 1% of the time
where the time goes in v5:
time: 37.6 us; the launch traced here: 37.5 us
  Pallas kernels  36.8 us (98%)
  between operations  0.64 us (2%)
    pallas_call x1, Pallas kernels, per_device(): pl.pallas_call(exchange, name='exchange', out_shape=(jax.ShapeDtypeStruct...  35.9 us
    pallas_call x1, Pallas kernels, per_device(): pl.pallas_call(store_all, name='store_all', out_shape=(jax.ShapeDtypeStru...  0.92 us

profile of v5, /device:TPU:1, one launch (start us, length us, event | category | flops | bytes accessed | tf_op | source)
XLA Modules:
  0.0 37.5 jit_solution(12224217628118183423)
XLA Ops:
  0.6 35.9 %exchange.1 = (f32[7,128,128]{2,1,0:T(8,128)S(1)}, s32[8,128]{1,0:T(8,128)S(1)}, f32[286,128]{1,0:T(8,128)S(1)}, f32[286,128]{1,0:T(8,128)S(1)}) custom-call(s32[256]{0:T(256)} %live_hbm.1, s32[8,256]{1,0:T(8,128)} %sends_hbm.1, s32[1,128]{1,0:T(1,128)} %bitcast.2, f32[3,128,128]{2,1,0:T(8,128)} %positions.1, f32[128,128]{1,0:T(8,128)} %charges.1, ...), custom_call_target="tpu_custom_call" | custom-call | tf_op jit(solution)/shard_map/exchange/pallas_call | solution.py:476
  36.6 0.9 %store_all.1 = (f32[3,128,128]{2,1,0:T(8,128)}, f32[128,128]{1,0:T(8,128)}, f32[3,128,128]{2,1,0:T(8,128)}, s32[1,128]{1,0:T(1,128)}, f32[286,128]{1,0:T(8,128)}, /*index=5*/f32[286,128]{1,0:T(8,128)}) custom-call(f32[7,128,128]{2,1,0:T(8,128)S(1)} %get-tuple-element.16.final, s32[8,128]{1,0:T(8,128)S(1)} %get-tuple-element.17.leaf_final, ...), custom_call_target="tpu_custom_call" | custom-call | tf_op jit(solution)/shard_map/store_all/pallas_call | solution.py:514
